TPU v7x, 16 devices: a whole 2x2x2 slice. The times are simulated.
16 devices in a mesh: row: 2 (over z), col: 8 (over y, x, core).
Axes of the slice: x: 2, y: 2, z: 2, core: 2. Of those that a mesh axis runs over, the one named last changes fastest.
Arguments:
- v_panels: float32 [4096, 4096], P('row', 'col')
- t_factors: float32 [128, 32, 32], replicated
- z_vecs: float32 [4096, 2048], P(None, ('col', 'row'))
- chol_low: float32 [4096, 4096], P('row', 'col')
Outputs:
- output: float32 [4096, 2048], P('row', 'col')
All inputs are finite; a program needn't handle non-finite values.
Results may differ from a plain program's by a relative error of at most 0.001.
Values sent between devices are 32-bit elements.
A program may use at most 1 GiB of HBM per device.

v0:
```python
import jax
import jax.numpy as jnp
from jax import lax
from jax.sharding import PartitionSpec as P

FULL_PREC = lax.Precision.HIGHEST


def solution(mesh):
    row_grid = mesh.shape['row']
    col_grid = mesh.shape['col']

    def local_work(v_loc, t_all, z_loc, l_loc):
        num_panels = t_all.shape[0]
        panel_w = t_all.shape[1]
        rounds = num_panels // col_grid
        row_id = lax.axis_index('row')
        x_start = lax.all_to_all(z_loc, 'row', 0, 1, tiled=True)
        eye_blk = jnp.eye(panel_w, dtype=x_start.dtype)

        def house_round(outer_idx, x_mat):
            round_idx = rounds - 1 - outer_idx
            own_pan = lax.dynamic_slice_in_dim(v_loc, round_idx * panel_w, panel_w, axis=1)
            gathered = lax.all_gather(own_pan, 'col')

            def house_panel(inner_idx, x_cur):
                slot_idx = col_grid - 1 - inner_idx
                v_pan = lax.dynamic_index_in_dim(gathered, slot_idx, 0, keepdims=False)
                t_pan = lax.dynamic_index_in_dim(t_all, round_idx * col_grid + slot_idx, 0, keepdims=False)
                w_part = jnp.einsum('nb,nk->bk', v_pan, x_cur, preferred_element_type=jnp.float32, precision=FULL_PREC)
                w_mat = lax.psum(w_part, 'row')
                y_mat = jnp.dot(t_pan, w_mat, preferred_element_type=jnp.float32, precision=FULL_PREC)
                return x_cur - jnp.dot(v_pan, y_mat, preferred_element_type=jnp.float32, precision=FULL_PREC)

            return lax.fori_loop(0, col_grid, house_panel, x_mat)

        x_done = lax.fori_loop(0, rounds, house_round, x_start)

        def solve_round(outer_idx, y_mat):
            round_idx = rounds - 1 - outer_idx
            own_pan = lax.dynamic_slice_in_dim(l_loc, round_idx * panel_w, panel_w, axis=1)
            gathered = lax.all_gather(own_pan, 'col')

            def solve_panel(inner_idx, y_cur):
                slot_idx = col_grid - 1 - inner_idx
                block_idx = round_idx * col_grid + slot_idx
                is_owner = (block_idx % row_grid) == row_id
                row_start = (block_idx // row_grid) * panel_w
                l_pan = lax.dynamic_index_in_dim(gathered, slot_idx, 0, keepdims=False)
                x_blk = lax.dynamic_slice_in_dim(x_done, row_start, panel_w, axis=0)
                w_part = jnp.einsum('nb,nk->bk', l_pan, y_cur, preferred_element_type=jnp.float32, precision=FULL_PREC) - jnp.where(is_owner, x_blk, 0.0)
                rhs_blk = -lax.psum(w_part, 'row')
                diag_blk = jnp.where(is_owner, lax.dynamic_slice_in_dim(l_pan, row_start, panel_w, axis=0), eye_blk)
                sol_blk = lax.linalg.triangular_solve(diag_blk, rhs_blk, left_side=True, lower=True, transpose_a=True)
                old_blk = lax.dynamic_slice_in_dim(y_cur, row_start, panel_w, axis=0)
                return lax.dynamic_update_slice_in_dim(y_cur, jnp.where(is_owner, sol_blk, old_blk), row_start, axis=0)

            return lax.fori_loop(0, col_grid, solve_panel, y_mat)

        return lax.fori_loop(0, rounds, solve_round, jnp.zeros_like(x_done))

    return jax.shard_map(local_work, mesh=mesh, in_specs=(P('row', 'col'), P(), P(None, ('col', 'row')), P('row', 'col')), out_specs=P('row', 'col'), check_vma=False)
```

profile of v0, /device:TPU:0, one launch (start us, length us, event | category | flops | bytes accessed | tf_op | source)
XLA Modules:
  0.0 5838.5 jit_solution(16012742620813535528)
XLA Ops:
  40.6 2845.0 %while.91 = (s32[]{:T(128)}, f32[2048,256]{1,0:T(8,128)S(1)}, f32[2048,512]{1,0:T(8,128)}, f32[128,32,32]{2,1,0:T(8,128)}, s32[]{:T(128)}, /*index=5*/s32[]{:T(1...) while((s32[]{:T(128)}, f32[2048,256]{1,0:T(8,128)S(1)}, ...), condition=%wide.region_4.5_spmd, body=%wide.region_0.4_spmd.sunk | while | flops 406331392 | bytes 23282220 | solution.py:37
  93.8 124.8 %while.94 = (s32[]{:T(128)}, f32[2048,256]{1,0:T(8,128)S(1)}, f32[8,2048,32]{2,1,0:T(8,128)}, s32[]{:T(128)}, f32[128,32,32]{2,1,0:T(8,128)}, /*index=5*/s32[]{:T(128)}, s32[]{:T(128)}, s32[]{:T(128)}, s32[]{:T(128)}, s32[]{:T(128)}) while((s32[]{:T(128)}, f32[2048,256]{1,0:T(8,128)S(1)}, f32[8,2048,32]{2,1,0:T(8,128)}, s32[]{:T(128)}, ...), condition=%wide.region_3.3_spmd, body=%wide.region_1.2_spmd.sunk | while | flops 406331392 | bytes 8601813 | solution.py:35
  982.8 124.9 %while.94 = (s32[]{:T(128)}, f32[2048,256]{1,0:T(8,128)S(1)}, f32[8,2048,32]{2,1,0:T(8,128)}, s32[]{:T(128)}, f32[128,32,32]{2,1,0:T(8,128)}, /*index=5*/s32[]{:T(128)}, s32[]{:T(128)}, s32[]{:T(128)}, s32[]{:T(128)}, s32[]{:T(128)}) while((s32[]{:T(128)}, f32[2048,256]{1,0:T(8,128)S(1)}, f32[8,2048,32]{2,1,0:T(8,128)}, s32[]{:T(128)}, ...), condition=%wide.region_3.3_spmd, body=%wide.region_1.2_spmd.sunk | while | flops 406331392 | bytes 8601813 | solution.py:35
  1871.8 124.9 %while.94 = (s32[]{:T(128)}, f32[2048,256]{1,0:T(8,128)S(1)}, f32[8,2048,32]{2,1,0:T(8,128)}, s32[]{:T(128)}, f32[128,32,32]{2,1,0:T(8,128)}, /*index=5*/s32[]{:T(128)}, s32[]{:T(128)}, s32[]{:T(128)}, s32[]{:T(128)}, s32[]{:T(128)}) while((s32[]{:T(128)}, f32[2048,256]{1,0:T(8,128)S(1)}, f32[8,2048,32]{2,1,0:T(8,128)}, s32[]{:T(128)}, ...), condition=%wide.region_3.3_spmd, body=%wide.region_1.2_spmd.sunk | while | flops 406331392 | bytes 8601813 | solution.py:35
  2227.4 124.9 %while.94 = (s32[]{:T(128)}, f32[2048,256]{1,0:T(8,128)S(1)}, f32[8,2048,32]{2,1,0:T(8,128)}, s32[]{:T(128)}, f32[128,32,32]{2,1,0:T(8,128)}, /*index=5*/s32[]{:T(128)}, s32[]{:T(128)}, s32[]{:T(128)}, s32[]{:T(128)}, s32[]{:T(128)}) while((s32[]{:T(128)}, f32[2048,256]{1,0:T(8,128)S(1)}, f32[8,2048,32]{2,1,0:T(8,128)}, s32[]{:T(128)}, ...), condition=%wide.region_3.3_spmd, body=%wide.region_1.2_spmd.sunk | while | flops 406331392 | bytes 8601813 | solution.py:35
  2583.0 124.9 %while.94 = (s32[]{:T(128)}, f32[2048,256]{1,0:T(8,128)S(1)}, f32[8,2048,32]{2,1,0:T(8,128)}, s32[]{:T(128)}, f32[128,32,32]{2,1,0:T(8,128)}, /*index=5*/s32[]{:T(128)}, s32[]{:T(128)}, s32[]{:T(128)}, s32[]{:T(128)}, s32[]{:T(128)}) while((s32[]{:T(128)}, f32[2048,256]{1,0:T(8,128)S(1)}, f32[8,2048,32]{2,1,0:T(8,128)}, s32[]{:T(128)}, ...), condition=%wide.region_3.3_spmd, body=%wide.region_1.2_spmd.sunk | while | flops 406331392 | bytes 8601813 | solution.py:35
  2760.7 124.9 %while.94 = (s32[]{:T(128)}, f32[2048,256]{1,0:T(8,128)S(1)}, f32[8,2048,32]{2,1,0:T(8,128)}, s32[]{:T(128)}, f32[128,32,32]{2,1,0:T(8,128)}, /*index=5*/s32[]{:T(128)}, s32[]{:T(128)}, s32[]{:T(128)}, s32[]{:T(128)}, s32[]{:T(128)}) while((s32[]{:T(128)}, f32[2048,256]{1,0:T(8,128)S(1)}, f32[8,2048,32]{2,1,0:T(8,128)}, s32[]{:T(128)}, ...), condition=%wide.region_3.3_spmd, body=%wide.region_1.2_spmd.sunk | while | flops 406331392 | bytes 8601813 | solution.py:35
  2887.1 2944.9 %while.93 = (s32[]{:T(128)}, f32[2048,256]{1,0:T(8,128)}, f32[2048,512]{1,0:T(8,128)}, s32[]{:T(128)}, f32[2048,256]{1,0:T(8,128)S(1)}, /*index=5*/s32[]{:T(128)...) while((s32[]{:T(128)}, f32[2048,256]{1,0:T(8,128)}, ...), condition=%wide.region_9.10_spmd.clone, body=%wide.region_5.9_spmd.clone.sunk | while | flops 204518432 | bytes 18076592 | solution.py:60
  2940.0 131.1 %while.95 = (s32[]{:T(128)}, f32[2048,256]{1,0:T(8,128)}, s32[]{:T(128)}, s32[]{:T(128)}, f32[8,2048,32]{2,1,0:T(8,128)}, /*index=5*/f32[32,32]{1,0:T(8,128)S(1)...) while((s32[]{:T(128)}, f32[2048,256]{1,0:T(8,128)}, ...), condition=%wide.region_8.8_spmd, body=%wide.region_6.7_spmd.sunk | while | flops 204516384 | bytes 3392000 | solution.py:58
  3124.0 131.1 %while.95 = (s32[]{:T(128)}, f32[2048,256]{1,0:T(8,128)}, s32[]{:T(128)}, s32[]{:T(128)}, f32[8,2048,32]{2,1,0:T(8,128)}, /*index=5*/f32[32,32]{1,0:T(8,128)S(1)...) while((s32[]{:T(128)}, f32[2048,256]{1,0:T(8,128)}, ...), condition=%wide.region_8.8_spmd, body=%wide.region_6.7_spmd.sunk | while | flops 204516384 | bytes 3392000 | solution.py:58
  3308.1 131.1 %while.95 = (s32[]{:T(128)}, f32[2048,256]{1,0:T(8,128)}, s32[]{:T(128)}, s32[]{:T(128)}, f32[8,2048,32]{2,1,0:T(8,128)}, /*index=5*/f32[32,32]{1,0:T(8,128)S(1)...) while((s32[]{:T(128)}, f32[2048,256]{1,0:T(8,128)}, ...), condition=%wide.region_8.8_spmd, body=%wide.region_6.7_spmd.sunk | while | flops 204516384 | bytes 3392000 | solution.py:58
  3492.1 131.1 %while.95 = (s32[]{:T(128)}, f32[2048,256]{1,0:T(8,128)}, s32[]{:T(128)}, s32[]{:T(128)}, f32[8,2048,32]{2,1,0:T(8,128)}, /*index=5*/f32[32,32]{1,0:T(8,128)S(1)...) while((s32[]{:T(128)}, f32[2048,256]{1,0:T(8,128)}, ...), condition=%wide.region_8.8_spmd, body=%wide.region_6.7_spmd.sunk | while | flops 204516384 | bytes 3392000 | solution.py:58
  3676.2 131.1 %while.95 = (s32[]{:T(128)}, f32[2048,256]{1,0:T(8,128)}, s32[]{:T(128)}, s32[]{:T(128)}, f32[8,2048,32]{2,1,0:T(8,128)}, /*index=5*/f32[32,32]{1,0:T(8,128)S(1)...) while((s32[]{:T(128)}, f32[2048,256]{1,0:T(8,128)}, ...), condition=%wide.region_8.8_spmd, body=%wide.region_6.7_spmd.sunk | while | flops 204516384 | bytes 3392000 | solution.py:58
  3860.3 131.1 %while.95 = (s32[]{:T(128)}, f32[2048,256]{1,0:T(8,128)}, s32[]{:T(128)}, s32[]{:T(128)}, f32[8,2048,32]{2,1,0:T(8,128)}, /*index=5*/f32[32,32]{1,0:T(8,128)S(1)...) while((s32[]{:T(128)}, f32[2048,256]{1,0:T(8,128)}, ...), condition=%wide.region_8.8_spmd, body=%wide.region_6.7_spmd.sunk | while | flops 204516384 | bytes 3392000 | solution.py:58
  4044.3 131.1 %while.95 = (s32[]{:T(128)}, f32[2048,256]{1,0:T(8,128)}, s32[]{:T(128)}, s32[]{:T(128)}, f32[8,2048,32]{2,1,0:T(8,128)}, /*index=5*/f32[32,32]{1,0:T(8,128)S(1)...) while((s32[]{:T(128)}, f32[2048,256]{1,0:T(8,128)}, ...), condition=%wide.region_8.8_spmd, body=%wide.region_6.7_spmd.sunk | while | flops 204516384 | bytes 3392000 | solution.py:58
  4228.4 131.1 %while.95 = (s32[]{:T(128)}, f32[2048,256]{1,0:T(8,128)}, s32[]{:T(128)}, s32[]{:T(128)}, f32[8,2048,32]{2,1,0:T(8,128)}, /*index=5*/f32[32,32]{1,0:T(8,128)S(1)...) while((s32[]{:T(128)}, f32[2048,256]{1,0:T(8,128)}, ...), condition=%wide.region_8.8_spmd, body=%wide.region_6.7_spmd.sunk | while | flops 204516384 | bytes 3392000 | solution.py:58
  4412.4 131.1 %while.95 = (s32[]{:T(128)}, f32[2048,256]{1,0:T(8,128)}, s32[]{:T(128)}, s32[]{:T(128)}, f32[8,2048,32]{2,1,0:T(8,128)}, /*index=5*/f32[32,32]{1,0:T(8,128)S(1)...) while((s32[]{:T(128)}, f32[2048,256]{1,0:T(8,128)}, ...), condition=%wide.region_8.8_spmd, body=%wide.region_6.7_spmd.sunk | while | flops 204516384 | bytes 3392000 | solution.py:58
  4596.5 131.1 %while.95 = (s32[]{:T(128)}, f32[2048,256]{1,0:T(8,128)}, s32[]{:T(128)}, s32[]{:T(128)}, f32[8,2048,32]{2,1,0:T(8,128)}, /*index=5*/f32[32,32]{1,0:T(8,128)S(1)...) while((s32[]{:T(128)}, f32[2048,256]{1,0:T(8,128)}, ...), condition=%wide.region_8.8_spmd, body=%wide.region_6.7_spmd.sunk | while | flops 204516384 | bytes 3392000 | solution.py:58
  4780.5 131.1 %while.95 = (s32[]{:T(128)}, f32[2048,256]{1,0:T(8,128)}, s32[]{:T(128)}, s32[]{:T(128)}, f32[8,2048,32]{2,1,0:T(8,128)}, /*index=5*/f32[32,32]{1,0:T(8,128)S(1)...) while((s32[]{:T(128)}, f32[2048,256]{1,0:T(8,128)}, ...), condition=%wide.region_8.8_spmd, body=%wide.region_6.7_spmd.sunk | while | flops 204516384 | bytes 3392000 | solution.py:58
  4964.6 131.1 %while.95 = (s32[]{:T(128)}, f32[2048,256]{1,0:T(8,128)}, s32[]{:T(128)}, s32[]{:T(128)}, f32[8,2048,32]{2,1,0:T(8,128)}, /*index=5*/f32[32,32]{1,0:T(8,128)S(1)...) while((s32[]{:T(128)}, f32[2048,256]{1,0:T(8,128)}, ...), condition=%wide.region_8.8_spmd, body=%wide.region_6.7_spmd.sunk | while | flops 204516384 | bytes 3392000 | solution.py:58
  5148.6 131.1 %while.95 = (s32[]{:T(128)}, f32[2048,256]{1,0:T(8,128)}, s32[]{:T(128)}, s32[]{:T(128)}, f32[8,2048,32]{2,1,0:T(8,128)}, /*index=5*/f32[32,32]{1,0:T(8,128)S(1)...) while((s32[]{:T(128)}, f32[2048,256]{1,0:T(8,128)}, ...), condition=%wide.region_8.8_spmd, body=%wide.region_6.7_spmd.sunk | while | flops 204516384 | bytes 3392000 | solution.py:58
  5332.7 131.1 %while.95 = (s32[]{:T(128)}, f32[2048,256]{1,0:T(8,128)}, s32[]{:T(128)}, s32[]{:T(128)}, f32[8,2048,32]{2,1,0:T(8,128)}, /*index=5*/f32[32,32]{1,0:T(8,128)S(1)...) while((s32[]{:T(128)}, f32[2048,256]{1,0:T(8,128)}, ...), condition=%wide.region_8.8_spmd, body=%wide.region_6.7_spmd.sunk | while | flops 204516384 | bytes 3392000 | solution.py:58
  5516.8 131.1 %while.95 = (s32[]{:T(128)}, f32[2048,256]{1,0:T(8,128)}, s32[]{:T(128)}, s32[]{:T(128)}, f32[8,2048,32]{2,1,0:T(8,128)}, /*index=5*/f32[32,32]{1,0:T(8,128)S(1)...) while((s32[]{:T(128)}, f32[2048,256]{1,0:T(8,128)}, ...), condition=%wide.region_8.8_spmd, body=%wide.region_6.7_spmd.sunk | while | flops 204516384 | bytes 3392000 | solution.py:58
  5700.8 131.1 %while.95 = (s32[]{:T(128)}, f32[2048,256]{1,0:T(8,128)}, s32[]{:T(128)}, s32[]{:T(128)}, f32[8,2048,32]{2,1,0:T(8,128)}, /*index=5*/f32[32,32]{1,0:T(8,128)S(1)...) while((s32[]{:T(128)}, f32[2048,256]{1,0:T(8,128)}, ...), condition=%wide.region_8.8_spmd, body=%wide.region_6.7_spmd.sunk | while | flops 204516384 | bytes 3392000 | solution.py:58
  (1314 shorter events, 7064.0 us)
Async XLA Ops:
  40.6 53.2 all-gather.10.cloned.1.call-start
  396.5 52.9 all-gather.10.cloned.1.call-start
  574.3 52.9 all-gather.10.cloned.1.call-start
  752.1 52.9 all-gather.10.cloned.1.call-start
  929.9 52.9 all-gather.10.cloned.1.call-start
  1285.4 52.9 all-gather.10.cloned.1.call-start
  1641.0 52.9 all-gather.10.cloned.1.call-start
  1818.8 52.9 all-gather.10.cloned.1.call-start
  2530.0 52.9 all-gather.10.cloned.1.call-start
  3071.1 52.9 all-gather.12.cloned.1.call-start
  3255.2 52.9 all-gather.12.cloned.1.call-start
  3439.2 52.9 all-gather.12.cloned.1.call-start
  3623.3 52.9 all-gather.12.cloned.1.call-start
  3807.3 52.9 all-gather.12.cloned.1.call-start
  3991.4 52.9 all-gather.12.cloned.1.call-start
  4175.4 52.9 all-gather.12.cloned.1.call-start
  4359.5 52.9 all-gather.12.cloned.1.call-start
  4543.5 52.9 all-gather.12.cloned.1.call-start
  4727.6 52.9 all-gather.12.cloned.1.call-start
  4911.7 52.9 all-gather.12.cloned.1.call-start
  5095.7 52.9 all-gather.12.cloned.1.call-start
  5279.8 52.9 all-gather.12.cloned.1.call-start
  5463.8 52.9 all-gather.12.cloned.1.call-start
  5647.9 52.9 all-gather.12.cloned.1.call-start
  (10 other events, 458.4 us)
Sparse Core Ops, SparseCore 0:
  43.4 50.3 all-gather.9
  221.4 50.1 all-gather.9
  399.2 50.1 all-gather.9
  577.0 50.1 all-gather.9
  754.8 50.1 all-gather.9
  932.6 50.1 all-gather.9
  1288.2 50.1 all-gather.9
  1466.0 50.1 all-gather.9
  1643.8 50.1 all-gather.9
  1821.6 50.1 all-gather.9
  2177.2 50.1 all-gather.9
  2532.8 50.1 all-gather.9
  3073.9 50.1 all-gather.11
  3257.9 50.1 all-gather.11
  3442.0 50.1 all-gather.11
  3626.0 50.1 all-gather.11
  3810.1 50.1 all-gather.11
  3994.1 50.1 all-gather.11
  4178.2 50.1 all-gather.11
  4362.2 50.1 all-gather.11
  4730.4 50.1 all-gather.11
  4914.4 50.1 all-gather.11
  5282.5 50.1 all-gather.11
  5466.6 50.1 all-gather.11
  (8 shorter events, 400.6 us)
where the time goes:
time: 5880 us; the launch traced here: 5840 us
  blocking collectives  2020 us (34%)
  matrix products  1670 us (28%)
  waiting for transfers between devices  1630 us (28%)
  other arithmetic  406 us (7%)
  local copies, waits for them, and re-layouts  90.4 us (2%)
    psum x128, blocking collectives, house_panel(): w_mat = lax.psum(w_part, 'row')  1010 us
    psum x128, blocking collectives, solve_panel(): rhs_blk = -lax.psum(w_part, 'row')  1010 us
    all_gather x16, waiting for transfers between devices, house_round(): gathered = lax.all_gather(own_pan, 'col')  805 us
    all_gather x16, waiting for transfers between devices, solve_round(): gathered = lax.all_gather(own_pan, 'col')  804 us
    dot_general x128, matrix products, solve_panel(): jnp.einsum('nb,nk->bk', l_pan, y_cur, preferred_element_type=jnp.float32,...  486 us
    dot_general x128, matrix products, house_panel(): jnp.dot(v_pan, y_mat, preferred_element_type=jnp.float32, precision=FULL_...  476 us
    another operation x256, other arithmetic, solve_panel(): lax.linalg.triangular_solve(diag_blk, rhs_blk, left_side=True, lower=True...  406 us
    dot_general x128, matrix products, house_panel(): jnp.einsum('nb,nk->bk', v_pan, x_cur, preferred_element_type=jnp.float32,...  394 us
  transfers between devices with their start and end apart: 33, of which 33 were waited for; matrix products, arithmetic and copies ran while one was open for 0% of the time, Pallas kernels for 0%

commit v1 on v0

v1 whole, which is shorter than its diff:
```python
import functools

import jax
import jax.numpy as jnp
from jax import lax
from jax.experimental import pallas as pl
from jax.experimental.pallas import tpu as pltpu
from jax.sharding import PartitionSpec as P

HI = lax.Precision.HIGHEST
MESH = pl.DeviceIdType.MESH
F32 = jnp.float32

PW = 32
NR = 16
NTILE = NR * (NR + 1) // 2
PARTS = 3
PART_LANES = 256
CHUNK_TILES = PARTS * PART_LANES // 128
CHUNK_LANES = CHUNK_TILES * 128
NCH = -(-2 * NTILE // CHUNK_TILES)
LANES = NCH * CHUNK_LANES
LAG = 2
ORDER = [7, 6, 5, 4, 3, 2, 1, 0]


def pos(c):
    return (c % 2) * 4 + c // 2


def dot(a, b):
    return lax.dot_general(a, b, (((1,), (0,)), ((), ())), precision=HI, preferred_element_type=F32)


def dot_nt(a, b):
    return lax.dot_general(a, b, (((1,), (1,)), ((), ())), precision=HI, preferred_element_type=F32)


def aligned(i, m=128):
    return pl.multiple_of(i * m, m)


def body(p_ref, t_ref, z_ref, out_ref, g_ref, stage, tblk, xt, gv, w_acc, s_acc, ybuf, yout, own_sem, in_sem, tile_sem, recv, send, ysem):
    z = lax.axis_index("row")
    c = lax.axis_index("col")
    xb = (c // 2) % 2
    yb = c // 4
    kb = c % 2
    steps = {"x": (2 - 4 * xb, 0), "y": (4 - 8 * yb, 0), "z": (0, 1 - 2 * z)}

    def device(dims):
        return z + sum(steps[d][1] for d in dims), c + sum(steps[d][0] for d in dims)

    def row_of(dims):
        zz, cc = device(dims)
        return pl.multiple_of(zz * 256 + ((cc % 2) * 4 + cc // 2) * 32, 32)

    partner = (z, c + 1 - 2 * kb)
    subsets = ["", "x", "y", "z", "xy", "yz", "xz", "xyz"]
    rows = {frozenset(s): row_of(s) for s in subsets}
    neigh = {d: device(d) for d in "xyz"}
    own = rows[frozenset()]

    barrier = pltpu.get_barrier_semaphore()
    for dev in (neigh["x"], neigh["y"], neigh["z"], partner):
        pl.semaphore_signal(barrier, inc=1, device_id=dev, device_id_type=MESH)
    pl.semaphore_wait(barrier, 4)

    ld_own = pltpu.make_async_copy(p_ref, stage, own_sem.at[0])
    ld_own.start()
    ld_z = pltpu.make_async_copy(z_ref, yout, in_sem.at[0])
    ld_z.start()
    ld_t = pltpu.make_async_copy(t_ref, tblk, in_sem.at[1])
    ld_t.start()

    def push(stg, chunk, sources, part, dim, first=False):
        lo = pl.multiple_of(chunk * CHUNK_LANES + part * PART_LANES, 128)
        for s in sources:
            row = rows[frozenset(s)]
            src = p_ref.at[:, pl.ds(lo, PART_LANES)] if first else g_ref.at[pl.ds(row, PW), pl.ds(lo, PART_LANES)]
            pltpu.make_async_remote_copy(
                src_ref=src,
                dst_ref=g_ref.at[pl.ds(row, PW), pl.ds(lo, PART_LANES)],
                send_sem=send.at[stg],
                recv_sem=recv.at[stg, chunk],
                device_id=neigh[dim],
                device_id_type=MESH,
            ).start()

    def wait_in(stg, chunk):
        n = PW * (1, 2, 4, 8)[stg]
        ref = g_ref.at[pl.ds(0, n), pl.ds(aligned(chunk, CHUNK_LANES), CHUNK_LANES)]
        pltpu.make_async_copy(ref, ref, recv.at[stg, chunk]).wait()

    rots = ["xyz", "yzx", "zxy"]

    def comm_step(i, _):
        @pl.when((i >= 3 * LAG) & (i < NCH + 3 * LAG))
        def _():
            ch = i - 3 * LAG
            wait_in(2, ch)
            for s in subsets:
                row = rows[frozenset(s)]
                ref = g_ref.at[pl.ds(row, PW), pl.ds(aligned(ch, CHUNK_LANES), CHUNK_LANES)]
                pltpu.make_async_remote_copy(
                    src_ref=ref, dst_ref=ref, send_sem=send.at[3], recv_sem=recv.at[3, ch], device_id=partner, device_id_type=MESH
                ).start()

        @pl.when((i >= 2 * LAG) & (i < NCH + 2 * LAG))
        def _():
            ch = i - 2 * LAG
            wait_in(1, ch)
            for p, r in enumerate(rots):
                push(2, ch, ["", r[0], r[1], r[0] + r[1]], p, r[2])

        @pl.when((i >= LAG) & (i < NCH + LAG))
        def _():
            ch = i - LAG
            wait_in(0, ch)
            for p, r in enumerate(rots):
                push(1, ch, ["", r[0]], p, r[1])

        @pl.when(i < NCH)
        def _():
            for p, r in enumerate(rots):
                push(0, i, [""], p, r[0], first=True)

        return 0

    def comm(lo, hi):
        lax.fori_loop(lo, hi, comm_step, 0)

    comm(0, LAG)
    ld_own.wait()
    st_own = pltpu.make_async_copy(stage, g_ref.at[pl.ds(own, PW), :], own_sem.at[1])
    st_own.start()
    st_own.wait()
    comm(LAG, 2 * LAG)

    ld_z.wait()

    def make_xt(b, _):
        for h in range(2):
            xt[b, :, h * 128 : (h + 1) * 128] = yout[h * NR + b].T
        return 0

    lax.fori_loop(0, NR, make_xt, 0)
    ld_t.wait()

    def tiles_before(t):
        ph = t // NR
        u = t % NR
        return ph * NTILE + u * (u + 1) // 2

    def chunks_for(t):
        return (tiles_before(t + 1) + CHUNK_TILES - 1) // CHUNK_TILES

    def steps_for(t):
        return jnp.minimum(chunks_for(t) + 3 * LAG, NCH + 3 * LAG)

    def fetch(t):
        slot = t % 2
        base = tiles_before(t)

        def one(j, _):
            for h in range(2):
                pltpu.make_async_copy(
                    g_ref.at[pl.ds(256 * h, 256), pl.ds(aligned(base + j), 128)],
                    gv.at[slot, j, :, pl.ds(128 * h, 128)],
                    tile_sem.at[slot, j],
                ).start()
            return 0

        lax.fori_loop(0, t % NR + 1, one, 0)

    def tile_wait(slot, j):
        pltpu.make_async_copy(gv.at[slot, j], gv.at[slot, j], tile_sem.at[slot, j]).wait()

    def arrive(t, prev):
        def one(ch, _):
            wait_in(3, ch)
            return 0

        lax.fori_loop(prev, chunks_for(t), one, 0)

    def eliminate(a_s, a_w):
        ybuf[...] = jnp.zeros_like(ybuf)
        for n, cc in enumerate(ORDER):
            q = pos(cc) * 32
            y = a_w[q : q + 32]
            if n:
                y = y - dot(a_s[q : q + 32], ybuf[...])
            ybuf[q : q + 32, :] = y

    def prefetch(t):
        @pl.when(t + 1 < 2 * NR)
        def _():
            comm(steps_for(t), steps_for(t + 1))
            arrive(t + 1, chunks_for(t))
            fetch(t + 1)

    comm(2 * LAG, steps_for(0))
    arrive(0, 0)
    fetch(0)

    def house(t, _):
        r = NR - 1 - t
        slot = t % 2
        prefetch(t)
        w_acc[...] = jnp.zeros_like(w_acc)
        s_acc[...] = jnp.zeros_like(s_acc)

        def gather(j, _):
            tile_wait(slot, j)
            g = gv[slot, j]
            w_acc[...] += dot_nt(xt[r + j], g)
            s_acc[...] += dot_nt(g, g)
            return 0

        lax.fori_loop(0, t + 1, gather, 0)
        tb = tblk[r]
        eliminate(dot(tb, s_acc[...]), dot(tb, w_acc[...].T))
        yt = ybuf[...].T

        def scatter(j, _):
            xt[r + j] -= dot(yt, gv[slot, j])
            return 0

        lax.fori_loop(0, t + 1, scatter, 0)
        return 0

    lax.fori_loop(0, NR, house, 0)

    row_ids = lax.broadcasted_iota(jnp.int32, (256, 256), 0) // 32
    col_ids = lax.broadcasted_iota(jnp.int32, (256, 256), 1) // 32
    other = neigh["z"]

    def solve(u, _):
        t = NR + u
        r = NR - 1 - u
        slot = t % 2
        prefetch(t)
        w_acc[...] = xt[r]
        tile_wait(slot, 0)

        def gather(j, _):
            tile_wait(slot, j)
            w_acc[...] -= dot_nt(xt[r + j], gv[slot, j])
            return 0

        lax.fori_loop(1, u + 1, gather, 0)
        d = gv[slot, 0]
        tb = jnp.where(row_ids == col_ids, d, 0.0)
        eliminate(dot(tb, d), dot(tb, w_acc[...].T))
        y = ybuf[...]
        yout[2 * r] = y[:128]
        yout[2 * r + 1] = y[128:]
        xt[r] = y.T
        dst = out_ref.at[pl.ds(aligned(r), 128), pl.ds(aligned(z), 128)]
        pltpu.make_async_copy(yout.at[2 * r + z], dst, ysem.at[0]).start()
        pltpu.make_async_remote_copy(
            src_ref=yout.at[2 * r + 1 - z], dst_ref=dst, send_sem=ysem.at[1], recv_sem=ysem.at[2], device_id=other, device_id_type=MESH
        ).start()
        return 0

    lax.fori_loop(0, NR, solve, 0)
    half = out_ref.at[:, pl.ds(0, 128)]
    for i in range(3):
        pltpu.make_async_copy(half, half, ysem.at[i]).wait()
    for stg, n in enumerate((1, 2, 4, 8)):
        ref = g_ref.at[pl.ds(0, n * PW), :]
        pltpu.make_async_copy(ref, ref, send.at[stg]).wait()


def back_transform(p, tblk, z):
    any_spec = pl.BlockSpec(memory_space=pl.ANY)
    return pl.pallas_call(
        body,
        out_shape=(jax.ShapeDtypeStruct((2048, 256), F32), jax.ShapeDtypeStruct((512, LANES), F32)),
        in_specs=[any_spec] * 3,
        out_specs=(any_spec, any_spec),
        scratch_shapes=[
            pltpu.VMEM((PW, LANES), F32),
            pltpu.VMEM((NR, 256, 256), F32),
            pltpu.VMEM((NR, 128, 256), F32),
            pltpu.VMEM((2, NR, 256, 256), F32),
            pltpu.VMEM((128, 256), F32),
            pltpu.VMEM((256, 256), F32),
            pltpu.VMEM((256, 128), F32),
            pltpu.VMEM((2 * NR, 128, 128), F32),
            pltpu.SemaphoreType.DMA((2,)),
            pltpu.SemaphoreType.DMA((2,)),
            pltpu.SemaphoreType.DMA((2, NR)),
            pltpu.SemaphoreType.DMA((4, NCH)),
            pltpu.SemaphoreType.DMA((4,)),
            pltpu.SemaphoreType.DMA((3,)),
        ],
        compiler_params=pltpu.CompilerParams(collective_id=0, has_side_effects=True, vmem_limit_bytes=60 << 20),
        name="back_transform",
    )(p, tblk, z)


def local_work(v_loc, t_all, z_loc, l_loc):
    c = lax.axis_index("col")
    z = lax.axis_index("row")
    t_pan = t_all.reshape(NR, 4, 2, PW, PW).transpose(0, 2, 1, 3, 4).reshape(NR, 8, PW, PW)
    tblk = (t_pan[:, :, :, None, :] * jnp.eye(8, dtype=F32)[None, :, None, :, None]).reshape(NR, 256, 256)

    lt = l_loc.T
    sub = (c // 2) * PW
    diag = jnp.stack([lax.dynamic_slice(l_loc, (128 * r + sub, PW * r), (PW, PW)) for r in range(NR)])
    eye = jnp.broadcast_to(jnp.eye(PW, dtype=F32), diag.shape)
    mine = (c % 2) == z
    diag = jnp.where(mine, diag, eye)
    inv_t = jnp.swapaxes(lax.linalg.triangular_solve(diag, eye, left_side=True, lower=True), 1, 2)

    def stream(mat):
        return [mat[PW * r : PW * (r + 1), 128 * r :] for r in range(NR - 1, -1, -1)]

    l_parts = []
    for r in range(NR - 1, -1, -1):
        strip = lt[PW * r : PW * (r + 1), 128 * r :]
        first = strip[:, :128]
        first = jnp.where(mine, lax.dynamic_update_slice(first, inv_t[r], (0, sub)), first)
        l_parts.append(first)
        if r < NR - 1:
            l_parts.append(strip[:, 128:])
    pad = jnp.zeros((PW, LANES - 2 * NTILE * 128), F32)
    p = jnp.concatenate(stream(v_loc.T) + l_parts + [pad], axis=1)
    y, _ = back_transform(p, tblk, z_loc.reshape(2 * NR, 128, 128))
    return y


def solution(mesh):
    return jax.shard_map(
        local_work,
        mesh=mesh,
        in_specs=(P("row", "col"), P(), P(None, ("col", "row")), P("row", "col")),
        out_specs=P("row", "col"),
        check_vma=False,
    )
```

time: 5880 us -> 528 us (0.09)
  blocking collectives: 2020 us -> 0 us
  matrix products: 1670 us -> 0.39 us
  waiting for transfers between devices: 1630 us -> 0 us
  Pallas kernels: 0 us -> 367 us
  other arithmetic: 406 us -> 44.4 us
    psum x256 -> x0, blocking collectives: 2020 us -> none  [the longest x128 1010 us: house_panel(): w_mat = lax.psum(w_part, 'row')]
    all_gather x32 -> x0, waiting for transfers between devices: 1610 us -> none  [the longest x16 805 us: house_round(): gathered = lax.all_gather(own_pan, 'col')]
    dot_general x512 -> x0, matrix products: 1470 us -> none  [the longest x128 486 us: solve_panel(): jnp.einsum('nb,nk->bk', l_pan, y_cur, preferred_element_type=jnp.float32,...]
    pallas_call x0 -> x1, Pallas kernels: none -> 367 us  [back_transform(): pl.pallas_call(body, out_shape=(jax.ShapeDtypeStruct((2048, 256), F32), j...]
    another operation x256 -> x3, other arithmetic: 406 us -> 39.4 us  [local_work(): lax.linalg.triangular_solve(diag, eye, left_side=True, lower=True)]
    another operation x128 -> x1, matrix products: 197 us -> 0.39 us  [local_work(): lax.linalg.triangular_solve(diag, eye, left_side=True, lower=True)]
    unnamed x2 -> x67, local copies, waits for them, and re-layouts: 0.01 us -> 84.7 us
    dynamic_slice x32 -> x0, local copies, waits for them, and re-layouts: 82.3 us -> none  [the longest x16 41.7 us: solve_round(): lax.dynamic_slice_in_dim(l_loc, round_idx * panel_w, panel_w, axis=1)]
  transfers between devices with their start and end apart: 33 -> 0, of which waited for: 33 -> 0; matrix products, arithmetic and copies ran while one was open for 0% -> 0% of each run, Pallas kernels for 0% -> 0%
where the time goes in v1:
time: 528 us; the launch traced here: 525 us
  Pallas kernels  367 us (70%)
  local copies, waits for them, and re-layouts  113 us (21%)
  other arithmetic  44.4 us (8%)
    pallas_call x1, Pallas kernels, back_transform(): pl.pallas_call(body, out_shape=(jax.ShapeDtypeStruct((2048, 256), F32), j...  367 us
    unnamed x67, local copies, waits for them, and re-layouts  84.7 us
    another operation x3, other arithmetic, local_work(): lax.linalg.triangular_solve(diag, eye, left_side=True, lower=True)  39.4 us
    mul x4, local copies, waits for them, and re-layouts, local_work(): t_pan[:, :, :, None, :] * jnp.eye(8, dtype=F32)[None, :, None, :, None]  19.7 us

profile of v1, /device:TPU:0, one launch (start us, length us, event | category | flops | bytes accessed | tf_op | source)
XLA Modules:
  0.0 525.3 jit_solution(6842655022269741012)
XLA Ops:
  12.6 39.4 %custom-call.3 = f32[16,1,32,32]{2,3,1,0:T(8,128)S(1)} custom-call(f32[16,1,32,32]{3,2,1,0:T(8,128)S(1)} %select_select_fusion), custom_call_target="InvertDiagBlocksLowerTriangular" | custom-call | tf_op jit(solution)/shard_map/triangular_solve | solution.py:315
  52.8 2.8 copy.13
  55.6 1.8 copy.14
  57.5 5.4 %copy.9 = f32[2048,512]{0,1:T(8,128)} copy(f32[2048,512]{1,0:T(8,128)} %param.4) | data formatting | bytes 8388608 | tf_op args[0]
  62.9 5.4 %copy.10 = f32[2048,512]{0,1:T(8,128)} copy(f32[2048,512]{1,0:T(8,128)} %param.7) | data formatting | bytes 8388608 | tf_op args[3]
  81.3 1.6 slice_dynamic-update-slice_fusion.14
  82.9 1.6 slice_dynamic-update-slice_fusion.12
  84.5 1.6 slice_dynamic-update-slice_fusion.10
  86.1 1.6 slice_dynamic-update-slice_fusion.8
  87.8 1.6 slice_dynamic-update-slice_fusion.6
  89.4 1.7 slice_dynamic-update-slice_fusion.4
  91.0 1.7 slice_dynamic-update-slice_fusion.2
  92.7 1.7 slice_dynamic-update-slice_fusion
  117.9 1.6 slice_dynamic-update-slice_fusion.11
  120.1 1.6 slice_dynamic-update-slice_fusion.9
  122.4 1.6 slice_dynamic-update-slice_fusion.7
  124.6 1.6 slice_dynamic-update-slice_fusion.5
  126.8 1.6 slice_dynamic-update-slice_fusion.3
  129.1 1.7 slice_dynamic-update-slice_fusion.1
  131.4 7.1 %mul.27 = f32[16,8,32,8,32]{4,3,2,1,0:T(8,128)} broadcast(f32[16,8,32,32]{3,2,1,0:T(8,128)S(1)} %bitcast.142), dimensions={0,1,2,4} | broadcast | bytes 4718592 | tf_op jit(solution)/shard_map/mul | solution.py:307
  138.5 12.2 %mul.28 = f32[16,256,256]{2,1,0:T(8,128)} reshape(f32[16,8,32,8,32]{4,3,2,1,0:T(8,128)} %mul.27) | data formatting | bytes 8388608 | tf_op jit(solution)/shard_map/mul | solution.py:307
  150.7 4.7 broadcast_multiply_fusion.t_ref
  155.5 366.8 %back_transform.1 = (f32[2048,256]{1,0:T(8,128)}, f32[512,35328]{1,0:T(8,128)}) custom-call(f32[32,35328]{1,0:T(8,128)} %constant_dynamic-update-slice_fusion.16.p_ref, f32[16,256,256]{2,1,0:T(8,128)} %broadcast_multiply_fusion.t_ref, f32[32,128,128]{2,1,0:T(8,128)} %bitcast.144), custom_call_target="tpu_custom_call" | custom-call | tf_op jit(solution)/shard_map/back_transform/pallas_call | solution.py:277
  522.3 3.0 copy.95
  (79 shorter events, 53.5 us)
Async XLA Ops:
  0.0 52.8 %copy-start = (f32[128,32,32]{0,2,1:T(8,128)S(1)}, f32[128,32,32]{0,2,1:T(8,128)}, u32[]{:S(2)}) copy-start(f32[128,32,32]{0,2,1:T(8,128)} %param.5) | copy-start | bytes 1572868

commit v2 on v1

--- a/solution.py
+++ b/solution.py
@@ -21,6 +21,8 @@
 NCH = -(-2 * NTILE // CHUNK_TILES)
 LANES = NCH * CHUNK_LANES
 LAG = 2
+FIXED, GATHER, SCATTER, SOLVE = 30, 6, 3, 3
+TOTAL_COST = 2 * NR * FIXED + NTILE * (GATHER + SCATTER + SOLVE)
 ORDER = [7, 6, 5, 4, 3, 2, 1, 0]
 
 
@@ -40,7 +42,7 @@
     return pl.multiple_of(i * m, m)
 
 
-def body(p_ref, t_ref, z_ref, out_ref, g_ref, stage, tblk, xt, gv, w_acc, s_acc, ybuf, yout, own_sem, in_sem, tile_sem, recv, send, ysem):
+def body(v_ref, l_ref, t_ref, z_ref, out_ref, g_ref, vin, lin, stage, tin, tb, xt, gv, w_acc, s_acc, ybuf, yout, own_sem, in_sem, tile_sem, recv, send, ysem):
     z = lax.axis_index("row")
     c = lax.axis_index("col")
     xb = (c // 2) % 2
@@ -61,26 +63,30 @@
     neigh = {d: device(d) for d in "xyz"}
     own = rows[frozenset()]
 
+    loads = {}
+    for n, (ref, dst) in enumerate(((v_ref, vin), (l_ref, lin))):
+        for cg in (3, 2, 1, 0):
+            part = (pl.ds(512 * cg, 2048 - 512 * cg), pl.ds(128 * cg, 128))
+            loads[n, cg] = pltpu.make_async_copy(ref.at[part], dst.at[part], in_sem.at[4 * n + cg])
+            loads[n, cg].start()
+    ld_z = pltpu.make_async_copy(z_ref, yout, in_sem.at[8])
+    ld_z.start()
+    ld_t = pltpu.make_async_copy(t_ref, tin, in_sem.at[9])
+    ld_t.start()
+
     barrier = pltpu.get_barrier_semaphore()
     for dev in (neigh["x"], neigh["y"], neigh["z"], partner):
         pl.semaphore_signal(barrier, inc=1, device_id=dev, device_id_type=MESH)
     pl.semaphore_wait(barrier, 4)
 
-    ld_own = pltpu.make_async_copy(p_ref, stage, own_sem.at[0])
-    ld_own.start()
-    ld_z = pltpu.make_async_copy(z_ref, yout, in_sem.at[0])
-    ld_z.start()
-    ld_t = pltpu.make_async_copy(t_ref, tblk, in_sem.at[1])
-    ld_t.start()
-
-    def push(stg, chunk, sources, part, dim, first=False):
+    def push(stg, chunk, sources, part, dim):
         lo = pl.multiple_of(chunk * CHUNK_LANES + part * PART_LANES, 128)
         for s in sources:
             row = rows[frozenset(s)]
-            src = p_ref.at[:, pl.ds(lo, PART_LANES)] if first else g_ref.at[pl.ds(row, PW), pl.ds(lo, PART_LANES)]
+            dst = g_ref.at[pl.ds(row, PW), pl.ds(lo, PART_LANES)]
             pltpu.make_async_remote_copy(
-                src_ref=src,
-                dst_ref=g_ref.at[pl.ds(row, PW), pl.ds(lo, PART_LANES)],
+                src_ref=dst if s else stage.at[:, pl.ds(lo, PART_LANES)],
+                dst_ref=dst,
                 send_sem=send.at[stg],
                 recv_sem=recv.at[stg, chunk],
                 device_id=neigh[dim],
@@ -99,11 +105,16 @@
         def _():
             ch = i - 3 * LAG
             wait_in(2, ch)
+            lanes = pl.ds(aligned(ch, CHUNK_LANES), CHUNK_LANES)
             for s in subsets:
-                row = rows[frozenset(s)]
-                ref = g_ref.at[pl.ds(row, PW), pl.ds(aligned(ch, CHUNK_LANES), CHUNK_LANES)]
+                dst = g_ref.at[pl.ds(rows[frozenset(s)], PW), lanes]
                 pltpu.make_async_remote_copy(
-                    src_ref=ref, dst_ref=ref, send_sem=send.at[3], recv_sem=recv.at[3, ch], device_id=partner, device_id_type=MESH
+                    src_ref=dst if s else stage.at[:, lanes],
+                    dst_ref=dst,
+                    send_sem=send.at[3],
+                    recv_sem=recv.at[3, ch],
+                    device_id=partner,
+                    device_id_type=MESH,
                 ).start()
 
         @pl.when((i >= 2 * LAG) & (i < NCH + 2 * LAG))
@@ -123,19 +134,94 @@
         @pl.when(i < NCH)
         def _():
             for p, r in enumerate(rots):
-                push(0, i, [""], p, r[0], first=True)
+                push(0, i, [""], p, r[0])
 
         return 0
 
     def comm(lo, hi):
         lax.fori_loop(lo, hi, comm_step, 0)
 
-    comm(0, LAG)
-    ld_own.wait()
-    st_own = pltpu.make_async_copy(stage, g_ref.at[pl.ds(own, PW), :], own_sem.at[1])
-    st_own.start()
-    st_own.wait()
-    comm(LAG, 2 * LAG)
+    def tile_index(base, r, b):
+        t = NR - 1 - r
+        return base + t * (t + 1) // 2 + b - r
+
+    def pack(src, base, cg):
+        def block(b, rounds):
+            x = src[pl.ds(aligned(b), 128), 128 * cg : 128 * cg + 128].T
+            for i in rounds:
+                stage[:, pl.ds(aligned(tile_index(base, 4 * cg + i, b)), 128)] = x[PW * i : PW * (i + 1)]
+
+        for i in range(4):
+            block(4 * cg + i, range(i + 1))
+
+        def rest(b, _):
+            block(b, range(4))
+            return 0
+
+        lax.fori_loop(4 * cg + 4, NR, rest, 0)
+
+    for cg in (3, 2, 1, 0):
+        loads[0, cg].wait()
+        pack(vin, 0, cg)
+        if cg == 3:
+            comm(0, 1)
+        elif cg == 2:
+            comm(1, 2)
+    stage[:, 2 * NTILE * 128 :] = jnp.zeros((PW, LANES - 2 * NTILE * 128), F32)
+    v_lanes = pl.ds(0, NTILE * 128)
+    st_v = pltpu.make_async_copy(stage.at[:, v_lanes], g_ref.at[pl.ds(own, PW), v_lanes], own_sem.at[0])
+    st_v.start()
+    comm(2, 3)
+    for cg in (3, 2, 1, 0):
+        loads[1, cg].wait()
+        pack(lin, NTILE, cg)
+    comm(3, 4)
+
+    row_ids = lax.broadcasted_iota(jnp.int32, (256, 256), 0)
+    col_ids = lax.broadcasted_iota(jnp.int32, (256, 256), 1)
+    lane_blk = lax.broadcasted_iota(jnp.int32, (PW, 128), 1) // PW
+
+    mine = kb == z
+    sub = c // 2
+
+    def move(x, to):
+        out = x
+        for a in range(4):
+            shift = (to - a) * PW % 128
+            out = jnp.where(sub == a, pltpu.roll(x, shift, 1) if shift else x, out)
+        return out
+
+    def invert(half, _):
+        s_acc[...] = jnp.zeros_like(s_acc)
+
+        def first(rr):
+            r = half * 8 + rr
+            return stage.at[:, pl.ds(aligned(tile_index(NTILE, r, r)), 128)]
+
+        for rr in range(8):
+            blk = jnp.where(lane_blk == rr % 4, move(first(rr)[...], rr % 4), 0.0)
+            s_acc[PW * rr : PW * (rr + 1), rr // 4 * 128 : rr // 4 * 128 + 128] = blk
+        eye = row_ids == col_ids
+        u = jnp.where(mine, s_acc[...], jnp.where(eye, 1.0, 0.0))
+        m = jnp.where(eye, 1.0 / jnp.where(eye, u, 1.0), 0.0)
+        for s in (1, 2, 4, 8, 16):
+            pair = (row_ids // (2 * s) == col_ids // (2 * s)) & (row_ids // s != col_ids // s)
+            m = m - dot(m, dot(jnp.where(pair, u, 0.0), m))
+        s_acc[...] = m
+        for rr in range(8):
+            x = s_acc[PW * rr : PW * (rr + 1), rr // 4 * 128 : rr // 4 * 128 + 128]
+            back = x
+            for a in range(4):
+                shift = (a - rr % 4) * PW % 128
+                back = jnp.where(sub == a, pltpu.roll(x, shift, 1) if shift else x, back)
+            ref = first(rr)
+            ref[...] = jnp.where((lane_blk == sub) & mine, back, ref[...])
+        return 0
+
+    lax.fori_loop(0, 2, lambda h, x: (invert(h, x), comm(4 + h, 5 + h))[0], 0)
+    l_lanes = pl.ds(NTILE * 128, LANES - NTILE * 128)
+    st_l = pltpu.make_async_copy(stage.at[:, l_lanes], g_ref.at[pl.ds(own, PW), l_lanes], own_sem.at[1])
+    st_l.start()
 
     ld_z.wait()
 
@@ -146,6 +232,7 @@
 
     lax.fori_loop(0, NR, make_xt, 0)
     ld_t.wait()
+    tb[...] = jnp.zeros_like(tb)
 
     def tiles_before(t):
         ph = t // NR
@@ -155,8 +242,11 @@
     def chunks_for(t):
         return (tiles_before(t + 1) + CHUNK_TILES - 1) // CHUNK_TILES
 
-    def steps_for(t):
-        return jnp.minimum(chunks_for(t) + 3 * LAG, NCH + 3 * LAG)
+    def paced(spent):
+        return 3 * LAG + 1 + spent * NCH // TOTAL_COST
+
+    def due(t, spent):
+        return jnp.minimum(jnp.maximum(chunks_for(t) + 3 * LAG, paced(spent)), NCH + 3 * LAG)
 
     def fetch(t):
         slot = t % 2
@@ -192,20 +282,33 @@
                 y = y - dot(a_s[q : q + 32], ybuf[...])
             ybuf[q : q + 32, :] = y
 
+    def h_cost(t):
+        return FIXED * t + (GATHER + SCATTER) * (t * (t + 1) // 2)
+
+    def l_cost(u):
+        return h_cost(NR) + FIXED * u + SOLVE * (u * (u + 1) // 2)
+
     def prefetch(t):
         @pl.when(t + 1 < 2 * NR)
         def _():
-            comm(steps_for(t), steps_for(t + 1))
             arrive(t + 1, chunks_for(t))
             fetch(t + 1)
 
-    comm(2 * LAG, steps_for(0))
+    st_v.wait()
+    comm(6, due(0, 0))
     arrive(0, 0)
     fetch(0)
+    st_l.wait()
 
     def house(t, _):
         r = NR - 1 - t
         slot = t % 2
+        n = t + 1
+        mid = n // 2
+        c0 = h_cost(t)
+        c1 = c0 + GATHER * mid
+        c2 = c0 + GATHER * n + FIXED
+        comm(jnp.where(t == 0, due(0, 0), due(t, c0)), due(t + 1, c0))
         prefetch(t)
         w_acc[...] = jnp.zeros_like(w_acc)
         s_acc[...] = jnp.zeros_like(s_acc)
@@ -217,28 +320,36 @@
             s_acc[...] += dot_nt(g, g)
             return 0
 
-        lax.fori_loop(0, t + 1, gather, 0)
-        tb = tblk[r]
-        eliminate(dot(tb, s_acc[...]), dot(tb, w_acc[...].T))
+        lax.fori_loop(0, mid, gather, 0)
+        comm(due(t + 1, c0), due(t + 1, c1))
+        lax.fori_loop(mid, n, gather, 0)
+        for cc in range(8):
+            q = pos(cc)
+            x = tin[8 * r + cc]
+            x = jnp.concatenate([x] * 4, axis=1)
+            tb[PW * q : PW * (q + 1), q // 4 * 128 : q // 4 * 128 + 128] = jnp.where(lane_blk == q % 4, x, 0.0)
+        tbv = tb[...]
+        eliminate(dot(tbv, s_acc[...]), dot(tbv, w_acc[...].T))
         yt = ybuf[...].T
+        comm(due(t + 1, c1), due(t + 1, c2))
 
         def scatter(j, _):
             xt[r + j] -= dot(yt, gv[slot, j])
             return 0
 
-        lax.fori_loop(0, t + 1, scatter, 0)
+        lax.fori_loop(0, n, scatter, 0)
+        comm(due(t + 1, c2), due(t + 1, h_cost(t + 1)))
         return 0
 
     lax.fori_loop(0, NR, house, 0)
 
-    row_ids = lax.broadcasted_iota(jnp.int32, (256, 256), 0) // 32
-    col_ids = lax.broadcasted_iota(jnp.int32, (256, 256), 1) // 32
     other = neigh["z"]
 
     def solve(u, _):
         t = NR + u
         r = NR - 1 - u
         slot = t % 2
+        comm(due(t, l_cost(u)), due(t + 1, l_cost(u)))
         prefetch(t)
         w_acc[...] = xt[r]
         tile_wait(slot, 0)
@@ -250,12 +361,13 @@
 
         lax.fori_loop(1, u + 1, gather, 0)
         d = gv[slot, 0]
-        tb = jnp.where(row_ids == col_ids, d, 0.0)
-        eliminate(dot(tb, d), dot(tb, w_acc[...].T))
+        tbv = jnp.where(row_ids // PW == col_ids // PW, d, 0.0)
+        eliminate(dot(tbv, d), dot(tbv, w_acc[...].T))
         y = ybuf[...]
         yout[2 * r] = y[:128]
         yout[2 * r + 1] = y[128:]
         xt[r] = y.T
+        comm(due(t + 1, l_cost(u)), due(t + 1, l_cost(u + 1)))
         dst = out_ref.at[pl.ds(aligned(r), 128), pl.ds(aligned(z), 128)]
         pltpu.make_async_copy(yout.at[2 * r + z], dst, ysem.at[0]).start()
         pltpu.make_async_remote_copy(
@@ -272,16 +384,19 @@
         pltpu.make_async_copy(ref, ref, send.at[stg]).wait()
 
 
-def back_transform(p, tblk, z):
+def back_transform(v, l, t, z):
     any_spec = pl.BlockSpec(memory_space=pl.ANY)
     return pl.pallas_call(
         body,
         out_shape=(jax.ShapeDtypeStruct((2048, 256), F32), jax.ShapeDtypeStruct((512, LANES), F32)),
-        in_specs=[any_spec] * 3,
+        in_specs=[any_spec] * 4,
         out_specs=(any_spec, any_spec),
         scratch_shapes=[
+            pltpu.VMEM((2048, 512), F32),
+            pltpu.VMEM((2048, 512), F32),
             pltpu.VMEM((PW, LANES), F32),
-            pltpu.VMEM((NR, 256, 256), F32),
+            pltpu.VMEM((8 * NR, PW, PW), F32),
+            pltpu.VMEM((256, 256), F32),
             pltpu.VMEM((NR, 128, 256), F32),
             pltpu.VMEM((2, NR, 256, 256), F32),
             pltpu.VMEM((128, 256), F32),
@@ -289,7 +404,7 @@
             pltpu.VMEM((256, 128), F32),
             pltpu.VMEM((2 * NR, 128, 128), F32),
             pltpu.SemaphoreType.DMA((2,)),
-            pltpu.SemaphoreType.DMA((2,)),
+            pltpu.SemaphoreType.DMA((10,)),
             pltpu.SemaphoreType.DMA((2, NR)),
             pltpu.SemaphoreType.DMA((4, NCH)),
             pltpu.SemaphoreType.DMA((4,)),
@@ -297,37 +412,11 @@
         ],
         compiler_params=pltpu.CompilerParams(collective_id=0, has_side_effects=True, vmem_limit_bytes=60 << 20),
         name="back_transform",
-    )(p, tblk, z)
+    )(v, l, t, z)
 
 
 def local_work(v_loc, t_all, z_loc, l_loc):
-    c = lax.axis_index("col")
-    z = lax.axis_index("row")
-    t_pan = t_all.reshape(NR, 4, 2, PW, PW).transpose(0, 2, 1, 3, 4).reshape(NR, 8, PW, PW)
-    tblk = (t_pan[:, :, :, None, :] * jnp.eye(8, dtype=F32)[None, :, None, :, None]).reshape(NR, 256, 256)
-
-    lt = l_loc.T
-    sub = (c // 2) * PW
-    diag = jnp.stack([lax.dynamic_slice(l_loc, (128 * r + sub, PW * r), (PW, PW)) for r in range(NR)])
-    eye = jnp.broadcast_to(jnp.eye(PW, dtype=F32), diag.shape)
-    mine = (c % 2) == z
-    diag = jnp.where(mine, diag, eye)
-    inv_t = jnp.swapaxes(lax.linalg.triangular_solve(diag, eye, left_side=True, lower=True), 1, 2)
-
-    def stream(mat):
-        return [mat[PW * r : PW * (r + 1), 128 * r :] for r in range(NR - 1, -1, -1)]
-
-    l_parts = []
-    for r in range(NR - 1, -1, -1):
-        strip = lt[PW * r : PW * (r + 1), 128 * r :]
-        first = strip[:, :128]
-        first = jnp.where(mine, lax.dynamic_update_slice(first, inv_t[r], (0, sub)), first)
-        l_parts.append(first)
-        if r < NR - 1:
-            l_parts.append(strip[:, 128:])
-    pad = jnp.zeros((PW, LANES - 2 * NTILE * 128), F32)
-    p = jnp.concatenate(stream(v_loc.T) + l_parts + [pad], axis=1)
-    y, _ = back_transform(p, tblk, z_loc.reshape(2 * NR, 128, 128))
+    y, _ = back_transform(v_loc, l_loc, t_all, z_loc.reshape(2 * NR, 128, 128))
     return y
 
 

time: 528 us -> 309 us (0.59)
  local copies, waits for them, and re-layouts: 113 us -> 6.89 us
  Pallas kernels: 367 us -> 302 us
  other arithmetic: 44.4 us -> 0 us
    unnamed x67 -> x2, local copies, waits for them, and re-layouts: 84.7 us -> 6.89 us
    pallas_call x1, Pallas kernels: 367 us -> 302 us  [back_transform(): pl.pallas_call(body, out_shape=(jax.ShapeDtypeStruct((2048, 256), F32), j...]
    another operation x3 -> x0, other arithmetic: 39.4 us -> none  [local_work(): lax.linalg.triangular_solve(diag, eye, left_side=True, lower=True)]
    mul x4 -> x0, local copies, waits for them, and re-layouts: 19.7 us -> none  [local_work(): t_pan[:, :, :, None, :] * jnp.eye(8, dtype=F32)[None, :, None, :, None]]
where the time goes in v2:
time: 309 us
  Pallas kernels  302 us (98%)
  local copies, waits for them, and re-layouts  6.89 us (2%)
    pallas_call x1, Pallas kernels, back_transform(): pl.pallas_call(body, out_shape=(jax.ShapeDtypeStruct((2048, 256), F32), j...  302 us
    unnamed x2, local copies, waits for them, and re-layouts  6.89 us

profile of v2, /device:TPU:0, one launch (start us, length us, event | category | flops | bytes accessed | tf_op | source)
XLA Modules:
  0.0 309.0 jit_solution(3048215467220427514)
XLA Ops:
  0.0 3.8 %copy.5.t_ref = f32[128,32,32]{2,1,0:T(8,128)} copy(f32[128,32,32]{0,2,1:T(8,128)} %param.5) | data formatting | bytes 1048576 | tf_op args[1]
  3.8 302.1 %back_transform.1 = (f32[2048,256]{1,0:T(8,128)}, f32[512,35328]{1,0:T(8,128)}) custom-call(f32[2048,512]{1,0:T(8,128)} %v_ref.1, f32[2048,512]{1,0:T(8,128)} %l_ref.1, f32[128,32,32]{2,1,0:T(8,128)} %copy.5.t_ref, f32[32,128,128]{2,1,0:T(8,128)} %bitcast.1), custom_call_target="tpu_custom_call" | custom-call | tf_op jit(solution)/shard_map/back_transform/pallas_call | solution.py:389
  306.0 3.0 copy.7

commit v3 on v2

--- a/solution.py
+++ b/solution.py
@@ -7,21 +7,21 @@
 from jax.experimental.pallas import tpu as pltpu
 from jax.sharding import PartitionSpec as P
 
-HI = lax.Precision.HIGHEST
 MESH = pl.DeviceIdType.MESH
 F32 = jnp.float32
 
 PW = 32
 NR = 16
 NTILE = NR * (NR + 1) // 2
-PARTS = 3
-PART_LANES = 256
-CHUNK_TILES = PARTS * PART_LANES // 128
+PART_TILES = (3, 4, 4)
+CHUNK_TILES = sum(PART_TILES)
 CHUNK_LANES = CHUNK_TILES * 128
 NCH = -(-2 * NTILE // CHUNK_TILES)
 LANES = NCH * CHUNK_LANES
 LAG = 2
-FIXED, GATHER, SCATTER, SOLVE = 30, 6, 3, 3
+LEAD = 1
+WIDTH_G, WIDTH_S, WIDTH_L = 4, 4, 4
+FIXED, GATHER, SCATTER, SOLVE = 23, 5, 2, 3
 TOTAL_COST = 2 * NR * FIXED + NTILE * (GATHER + SCATTER + SOLVE)
 ORDER = [7, 6, 5, 4, 3, 2, 1, 0]
 
@@ -30,19 +30,56 @@
     return (c % 2) * 4 + c // 2
 
 
+BF = jnp.bfloat16
+
+
+def split(x):
+    hi = x.astype(BF)
+    rest = x - hi.astype(F32)
+    mid = rest.astype(BF)
+    return hi, mid, (rest - mid.astype(F32)).astype(BF)
+
+
+def lhs(s):
+    hi, mid, lo = s
+    return jnp.concatenate([lo, hi, mid, mid, hi, hi], axis=1)
+
+
+def rhs(s, axis):
+    hi, mid, lo = s
+    return jnp.concatenate([hi, lo, mid, hi, mid, hi], axis=axis)
+
+
 def dot(a, b):
-    return lax.dot_general(a, b, (((1,), (0,)), ((), ())), precision=HI, preferred_element_type=F32)
-
-
-def dot_nt(a, b):
-    return lax.dot_general(a, b, (((1,), (1,)), ((), ())), precision=HI, preferred_element_type=F32)
+    return jnp.dot(lhs(split(a)), rhs(split(b), 0), preferred_element_type=F32)
+
+
+def dot_nt_split(pairs):
+    a = jnp.concatenate([lhs(p[0]) for p in pairs], axis=1)
+    b = jnp.concatenate([rhs(p[1], 1) for p in pairs], axis=1)
+    return lax.dot_general(a, b, (((1,), (1,)), ((), ())), preferred_element_type=F32)
+
+
+def tile_loop(lo, hi, width, fn):
+    full = (hi - lo) // width
+
+    def group(i, _):
+        fn([lo + width * i + k for k in range(width)])
+        return 0
+
+    def single(j, _):
+        fn([j])
+        return 0
+
+    lax.fori_loop(0, full, group, 0)
+    lax.fori_loop(lo + width * full, hi, single, 0)
 
 
 def aligned(i, m=128):
     return pl.multiple_of(i * m, m)
 
 
-def body(v_ref, l_ref, t_ref, z_ref, out_ref, g_ref, vin, lin, stage, tin, tb, xt, gv, w_acc, s_acc, ybuf, yout, own_sem, in_sem, tile_sem, recv, send, ysem):
+def body(v_ref, l_ref, t_ref, z_ref, out_ref, g_ref, vin, lin, stage, tin, tb, xt, gv, w_acc, s_acc, acc, ybuf, ysplit, gsplit, xsplit, yout, own_sem, in_sem, tile_sem, recv, send, ysem):
     z = lax.axis_index("row")
     c = lax.axis_index("col")
     xb = (c // 2) % 2
@@ -80,12 +117,13 @@
     pl.semaphore_wait(barrier, 4)
 
     def push(stg, chunk, sources, part, dim):
-        lo = pl.multiple_of(chunk * CHUNK_LANES + part * PART_LANES, 128)
+        lo = pl.multiple_of(chunk * CHUNK_LANES + sum(PART_TILES[:part]) * 128, 128)
+        lanes = pl.ds(lo, PART_TILES[part] * 128)
         for s in sources:
             row = rows[frozenset(s)]
-            dst = g_ref.at[pl.ds(row, PW), pl.ds(lo, PART_LANES)]
+            dst = g_ref.at[pl.ds(row, PW), lanes]
             pltpu.make_async_remote_copy(
-                src_ref=dst if s else stage.at[:, pl.ds(lo, PART_LANES)],
+                src_ref=dst if s else stage.at[:, lanes],
                 dst_ref=dst,
                 send_sem=send.at[stg],
                 recv_sem=recv.at[stg, chunk],
@@ -163,11 +201,10 @@
     for cg in (3, 2, 1, 0):
         loads[0, cg].wait()
         pack(vin, 0, cg)
-        if cg == 3:
-            comm(0, 1)
-        elif cg == 2:
-            comm(1, 2)
-    stage[:, 2 * NTILE * 128 :] = jnp.zeros((PW, LANES - 2 * NTILE * 128), F32)
+        if cg == 2:
+            comm(0, 2)
+    if LANES > 2 * NTILE * 128:
+        stage[:, 2 * NTILE * 128 :] = jnp.zeros((PW, LANES - 2 * NTILE * 128), F32)
     v_lanes = pl.ds(0, NTILE * 128)
     st_v = pltpu.make_async_copy(stage.at[:, v_lanes], g_ref.at[pl.ds(own, PW), v_lanes], own_sem.at[0])
     st_v.start()
@@ -243,10 +280,10 @@
         return (tiles_before(t + 1) + CHUNK_TILES - 1) // CHUNK_TILES
 
     def paced(spent):
-        return 3 * LAG + 1 + spent * NCH // TOTAL_COST
+        return 3 * LAG + LEAD + spent * NCH // TOTAL_COST
 
     def due(t, spent):
-        return jnp.minimum(jnp.maximum(chunks_for(t) + 3 * LAG, paced(spent)), NCH + 3 * LAG)
+        return jnp.minimum(jnp.maximum(jnp.maximum(chunks_for(t) + 3 * LAG + LEAD, paced(spent)), 6), NCH + 3 * LAG)
 
     def fetch(t):
         slot = t % 2
@@ -273,14 +310,20 @@
 
         lax.fori_loop(prev, chunks_for(t), one, 0)
 
-    def eliminate(a_s, a_w):
-        ybuf[...] = jnp.zeros_like(ybuf)
+    def eliminate(tbv, s_mat, w_mat):
+        a = dot(tbv, jnp.concatenate([s_mat, w_mat], axis=1))
+        a_s = lhs(split(a[:, :256]))
+        a_w = a[:, 256:]
+        ysplit[...] = jnp.zeros_like(ysplit)
         for n, cc in enumerate(ORDER):
-            q = pos(cc) * 32
-            y = a_w[q : q + 32]
+            q = pos(cc) * PW
+            y = a_w[q : q + PW]
             if n:
-                y = y - dot(a_s[q : q + 32], ybuf[...])
-            ybuf[q : q + 32, :] = y
+                y = y - jnp.dot(a_s[q : q + PW], rhs([ysplit[i] for i in range(3)], 0), preferred_element_type=F32)
+            ybuf[q : q + PW, :] = y
+            if n < 7:
+                for i, part in enumerate(split(y)):
+                    ysplit[i, q : q + PW, :] = part
 
     def h_cost(t):
         return FIXED * t + (GATHER + SCATTER) * (t * (t + 1) // 2)
@@ -304,40 +347,42 @@
         r = NR - 1 - t
         slot = t % 2
         n = t + 1
-        mid = n // 2
+        mid = n // 2 // WIDTH_G * WIDTH_G
         c0 = h_cost(t)
         c1 = c0 + GATHER * mid
         c2 = c0 + GATHER * n + FIXED
         comm(jnp.where(t == 0, due(0, 0), due(t, c0)), due(t + 1, c0))
         prefetch(t)
-        w_acc[...] = jnp.zeros_like(w_acc)
-        s_acc[...] = jnp.zeros_like(s_acc)
-
-        def gather(j, _):
-            tile_wait(slot, j)
-            g = gv[slot, j]
-            w_acc[...] += dot_nt(xt[r + j], g)
-            s_acc[...] += dot_nt(g, g)
-            return 0
-
-        lax.fori_loop(0, mid, gather, 0)
+        acc[...] = jnp.zeros_like(acc)
+
+        def gather(js):
+            pairs = []
+            for j in js:
+                tile_wait(slot, j)
+                gs = split(gv[slot, j])
+                for i, part in enumerate(gs):
+                    gsplit[j, i] = part
+                pairs.append(([jnp.concatenate(p, axis=0) for p in zip(split(xt[r + j]), gs)], gs))
+            acc[...] += dot_nt_split(pairs)
+
+        tile_loop(0, mid, WIDTH_G, gather)
         comm(due(t + 1, c0), due(t + 1, c1))
-        lax.fori_loop(mid, n, gather, 0)
+        tile_loop(mid, n, WIDTH_G, gather)
         for cc in range(8):
             q = pos(cc)
             x = tin[8 * r + cc]
             x = jnp.concatenate([x] * 4, axis=1)
             tb[PW * q : PW * (q + 1), q // 4 * 128 : q // 4 * 128 + 128] = jnp.where(lane_blk == q % 4, x, 0.0)
         tbv = tb[...]
-        eliminate(dot(tbv, s_acc[...]), dot(tbv, w_acc[...].T))
-        yt = ybuf[...].T
+        eliminate(tbv, acc[128:], acc[:128].T)
+        yt = lhs(split(ybuf[...].T))
         comm(due(t + 1, c1), due(t + 1, c2))
 
-        def scatter(j, _):
-            xt[r + j] -= dot(yt, gv[slot, j])
-            return 0
-
-        lax.fori_loop(0, n, scatter, 0)
+        def scatter(js):
+            for j in js:
+                xt[r + j] -= jnp.dot(yt, rhs([gsplit[j, i] for i in range(3)], 0), preferred_element_type=F32)
+
+        tile_loop(0, n, WIDTH_S, scatter)
         comm(due(t + 1, c2), due(t + 1, h_cost(t + 1)))
         return 0
 
@@ -350,23 +395,26 @@
         r = NR - 1 - u
         slot = t % 2
         comm(due(t, l_cost(u)), due(t + 1, l_cost(u)))
-        prefetch(t)
         w_acc[...] = xt[r]
         tile_wait(slot, 0)
 
-        def gather(j, _):
-            tile_wait(slot, j)
-            w_acc[...] -= dot_nt(xt[r + j], gv[slot, j])
-            return 0
-
-        lax.fori_loop(1, u + 1, gather, 0)
+        def gather(js):
+            pairs = []
+            for j in js:
+                tile_wait(slot, j)
+                pairs.append(([xsplit[r + j, i] for i in range(3)], split(gv[slot, j])))
+            w_acc[...] -= dot_nt_split(pairs)
+
+        tile_loop(1, u + 1, WIDTH_L, gather)
+        prefetch(t)
         d = gv[slot, 0]
         tbv = jnp.where(row_ids // PW == col_ids // PW, d, 0.0)
-        eliminate(dot(tbv, d), dot(tbv, w_acc[...].T))
+        eliminate(tbv, d, w_acc[...].T)
         y = ybuf[...]
         yout[2 * r] = y[:128]
         yout[2 * r + 1] = y[128:]
-        xt[r] = y.T
+        for i, part in enumerate(split(y.T)):
+            xsplit[r, i] = part
         comm(due(t + 1, l_cost(u)), due(t + 1, l_cost(u + 1)))
         dst = out_ref.at[pl.ds(aligned(r), 128), pl.ds(aligned(z), 128)]
         pltpu.make_async_copy(yout.at[2 * r + z], dst, ysem.at[0]).start()
@@ -401,7 +449,11 @@
             pltpu.VMEM((2, NR, 256, 256), F32),
             pltpu.VMEM((128, 256), F32),
             pltpu.VMEM((256, 256), F32),
+            pltpu.VMEM((384, 256), F32),
             pltpu.VMEM((256, 128), F32),
+            pltpu.VMEM((3, 256, 128), BF),
+            pltpu.VMEM((NR, 3, 256, 256), BF),
+            pltpu.VMEM((NR, 3, 128, 256), BF),
             pltpu.VMEM((2 * NR, 128, 128), F32),
             pltpu.SemaphoreType.DMA((2,)),
             pltpu.SemaphoreType.DMA((10,)),

time: 309 us -> 279 us (0.903)
  Pallas kernels: 302 us -> 272 us
    pallas_call x1, Pallas kernels: 302 us -> 272 us  [back_transform(): pl.pallas_call(body, out_shape=(jax.ShapeDtypeStruct((2048, 256), F32), j...]
where the time goes in v3:
time: 279 us
  Pallas kernels  272 us (97%)
  local copies, waits for them, and re-layouts  6.89 us (2%)
    pallas_call x1, Pallas kernels, back_transform(): pl.pallas_call(body, out_shape=(jax.ShapeDtypeStruct((2048, 256), F32), j...  272 us
    unnamed x2, local copies, waits for them, and re-layouts  6.89 us

profile of v3, /device:TPU:0, one launch (start us, length us, event | category | flops | bytes accessed | tf_op | source)
XLA Modules:
  0.0 278.7 jit_solution(9653744856715890172)
XLA Ops:
  0.0 3.8 %copy.5.t_ref = f32[128,32,32]{2,1,0:T(8,128)} copy(f32[128,32,32]{0,2,1:T(8,128)} %param.5) | data formatting | bytes 1048576 | tf_op args[1]
  3.8 271.8 %back_transform.1 = (f32[2048,256]{1,0:T(8,128)}, f32[512,35200]{1,0:T(8,128)}) custom-call(f32[2048,512]{1,0:T(8,128)} %v_ref.1, f32[2048,512]{1,0:T(8,128)} %l_ref.1, f32[128,32,32]{2,1,0:T(8,128)} %copy.5.t_ref, f32[32,128,128]{2,1,0:T(8,128)} %bitcast.1), custom_call_target="tpu_custom_call" | custom-call | tf_op jit(solution)/shard_map/back_transform/pallas_call | solution.py:437
  275.6 3.0 %copy.7 = f32[2048,256]{1,0:T(8,128)} copy(f32[2048,256]{1,0:T(8,128)} %get-tuple-element.6) | data formatting | bytes 4194304

commit v4 on v3

--- a/solution.py
+++ b/solution.py
@@ -19,9 +19,10 @@
 NCH = -(-2 * NTILE // CHUNK_TILES)
 LANES = NCH * CHUNK_LANES
 LAG = 2
+AHEAD = 1
 LEAD = 1
 WIDTH_G, WIDTH_S, WIDTH_L = 4, 4, 4
-FIXED, GATHER, SCATTER, SOLVE = 23, 5, 2, 3
+FIXED, GATHER, SCATTER, SOLVE = 46, 10, 4, 5
 TOTAL_COST = 2 * NR * FIXED + NTILE * (GATHER + SCATTER + SOLVE)
 ORDER = [7, 6, 5, 4, 3, 2, 1, 0]
 
@@ -116,18 +117,23 @@
         pl.semaphore_signal(barrier, inc=1, device_id=dev, device_id_type=MESH)
     pl.semaphore_wait(barrier, 4)
 
+    swap = {"x": "y", "y": "x", "z": "z"}
+
     def push(stg, chunk, sources, part, dim):
+        odd = chunk % 2
         lo = pl.multiple_of(chunk * CHUNK_LANES + sum(PART_TILES[:part]) * 128, 128)
         lanes = pl.ds(lo, PART_TILES[part] * 128)
+        (z0, c0), (z1, c1) = neigh[dim], neigh[swap[dim]]
         for s in sources:
-            row = rows[frozenset(s)]
+            r0, r1 = rows[frozenset(s)], rows[frozenset(swap[d] for d in s)]
+            row = r0 if r0 is r1 else pl.multiple_of(r0 + odd * (r1 - r0), 32)
             dst = g_ref.at[pl.ds(row, PW), lanes]
             pltpu.make_async_remote_copy(
                 src_ref=dst if s else stage.at[:, lanes],
                 dst_ref=dst,
                 send_sem=send.at[stg],
                 recv_sem=recv.at[stg, chunk],
-                device_id=neigh[dim],
+                device_id=neigh[dim] if dim == "z" else (z0, c0 + odd * (c1 - c0)),
                 device_id_type=MESH,
             ).start()
 
@@ -169,12 +175,15 @@
             for p, r in enumerate(rots):
                 push(1, ch, ["", r[0]], p, r[1])
 
-        @pl.when(i < NCH)
+        @pl.when(i + AHEAD < NCH)
         def _():
-            for p, r in enumerate(rots):
-                push(0, i, [""], p, r[0])
-
-        return 0
+            first_stage(i + AHEAD)
+
+        return 0
+
+    def first_stage(ch):
+        for p, r in enumerate(rots):
+            push(0, ch, [""], p, r[0])
 
     def comm(lo, hi):
         lax.fori_loop(lo, hi, comm_step, 0)
@@ -202,17 +211,19 @@
         loads[0, cg].wait()
         pack(vin, 0, cg)
         if cg == 2:
-            comm(0, 2)
+            lax.fori_loop(0, 3, lambda i, x: (first_stage(i), x)[1], 0)
+        if cg == 1:
+            lax.fori_loop(3, LAG + AHEAD, lambda i, x: (first_stage(i), x)[1], 0)
     if LANES > 2 * NTILE * 128:
         stage[:, 2 * NTILE * 128 :] = jnp.zeros((PW, LANES - 2 * NTILE * 128), F32)
     v_lanes = pl.ds(0, NTILE * 128)
     st_v = pltpu.make_async_copy(stage.at[:, v_lanes], g_ref.at[pl.ds(own, PW), v_lanes], own_sem.at[0])
     st_v.start()
-    comm(2, 3)
+    comm(LAG, LAG + 2)
     for cg in (3, 2, 1, 0):
         loads[1, cg].wait()
         pack(lin, NTILE, cg)
-    comm(3, 4)
+    comm(LAG + 2, LAG + 3)
 
     row_ids = lax.broadcasted_iota(jnp.int32, (256, 256), 0)
     col_ids = lax.broadcasted_iota(jnp.int32, (256, 256), 1)
@@ -255,7 +266,7 @@
             ref[...] = jnp.where((lane_blk == sub) & mine, back, ref[...])
         return 0
 
-    lax.fori_loop(0, 2, lambda h, x: (invert(h, x), comm(4 + h, 5 + h))[0], 0)
+    lax.fori_loop(0, 2, lambda h, x: (invert(h, x), comm(LAG + 3 + h, LAG + 4 + h))[0], 0)
     l_lanes = pl.ds(NTILE * 128, LANES - NTILE * 128)
     st_l = pltpu.make_async_copy(stage.at[:, l_lanes], g_ref.at[pl.ds(own, PW), l_lanes], own_sem.at[1])
     st_l.start()
@@ -283,7 +294,7 @@
         return 3 * LAG + LEAD + spent * NCH // TOTAL_COST
 
     def due(t, spent):
-        return jnp.minimum(jnp.maximum(jnp.maximum(chunks_for(t) + 3 * LAG + LEAD, paced(spent)), 6), NCH + 3 * LAG)
+        return jnp.minimum(jnp.maximum(jnp.maximum(chunks_for(t) + 3 * LAG + LEAD, paced(spent)), LAG + 5), NCH + 3 * LAG)
 
     def fetch(t):
         slot = t % 2
@@ -338,7 +349,7 @@
             fetch(t + 1)
 
     st_v.wait()
-    comm(6, due(0, 0))
+    comm(LAG + 5, due(0, 0))
     arrive(0, 0)
     fetch(0)
     st_l.wait()

time: 279 us -> 272 us (0.975)
  Pallas kernels: 272 us -> 265 us
    pallas_call x1, Pallas kernels: 272 us -> 265 us  [back_transform(): pl.pallas_call(body, out_shape=(jax.ShapeDtypeStruct((2048, 256), F32), j...]
where the time goes in v4:
time: 272 us
  Pallas kernels  265 us (97%)
  local copies, waits for them, and re-layouts  6.89 us (3%)
    pallas_call x1, Pallas kernels, back_transform(): pl.pallas_call(body, out_shape=(jax.ShapeDtypeStruct((2048, 256), F32), j...  265 us
    unnamed x2, local copies, waits for them, and re-layouts  6.89 us

profile of v4, /device:TPU:0, one launch (start us, length us, event | category | flops | bytes accessed | tf_op | source)
XLA Modules:
  0.0 272.2 jit_solution(14608462854047673898)
XLA Ops:
  0.0 3.8 %copy.5.t_ref = f32[128,32,32]{2,1,0:T(8,128)} copy(f32[128,32,32]{0,2,1:T(8,128)} %param.5) | data formatting | bytes 1048576 | tf_op args[1]
  3.8 265.3 %back_transform.1 = (f32[2048,256]{1,0:T(8,128)}, f32[512,35200]{1,0:T(8,128)}) custom-call(f32[2048,512]{1,0:T(8,128)} %v_ref.1, f32[2048,512]{1,0:T(8,128)} %l_ref.1, f32[128,32,32]{2,1,0:T(8,128)} %copy.5.t_ref, f32[32,128,128]{2,1,0:T(8,128)} %bitcast.1), custom_call_target="tpu_custom_call" | custom-call | tf_op jit(solution)/shard_map/back_transform/pallas_call | solution.py:448
  269.2 3.0 %copy.7 = f32[2048,256]{1,0:T(8,128)} copy(f32[2048,256]{1,0:T(8,128)} %get-tuple-element.6) | data formatting | bytes 4194304

commit v5 on v4

--- a/solution.py
+++ b/solution.py
@@ -426,12 +426,12 @@
         yout[2 * r + 1] = y[128:]
         for i, part in enumerate(split(y.T)):
             xsplit[r, i] = part
-        comm(due(t + 1, l_cost(u)), due(t + 1, l_cost(u + 1)))
         dst = out_ref.at[pl.ds(aligned(r), 128), pl.ds(aligned(z), 128)]
         pltpu.make_async_copy(yout.at[2 * r + z], dst, ysem.at[0]).start()
         pltpu.make_async_remote_copy(
             src_ref=yout.at[2 * r + 1 - z], dst_ref=dst, send_sem=ysem.at[1], recv_sem=ysem.at[2], device_id=other, device_id_type=MESH
         ).start()
+        comm(due(t + 1, l_cost(u)), due(t + 1, l_cost(u + 1)))
         return 0
 
     lax.fori_loop(0, NR, solve, 0)

time: 272 us -> 272 us (level)
  no operation moved by 1% of the time
where the time goes in v5:
time: 272 us
  Pallas kernels  265 us (97%)
  local copies, waits for them, and re-layouts  6.89 us (3%)
    pallas_call x1, Pallas kernels, back_transform(): pl.pallas_call(body, out_shape=(jax.ShapeDtypeStruct((2048, 256), F32), j...  265 us
    unnamed x2, local copies, waits for them, and re-layouts  6.89 us

profile of v5, /device:TPU:0, one launch (start us, length us, event | category | flops | bytes accessed | tf_op | source)
XLA Modules:
  0.0 272.2 jit_solution(4098302164267106289)
XLA Ops:
  0.0 3.8 %copy.5.t_ref = f32[128,32,32]{2,1,0:T(8,128)} copy(f32[128,32,32]{0,2,1:T(8,128)} %param.5) | data formatting | bytes 1048576 | tf_op args[1]
  3.8 265.3 %back_transform.1 = (f32[2048,256]{1,0:T(8,128)}, f32[512,35200]{1,0:T(8,128)}) custom-call(f32[2048,512]{1,0:T(8,128)} %v_ref.1, f32[2048,512]{1,0:T(8,128)} %l_ref.1, f32[128,32,32]{2,1,0:T(8,128)} %copy.5.t_ref, f32[32,128,128]{2,1,0:T(8,128)} %bitcast.1), custom_call_target="tpu_custom_call" | custom-call | tf_op jit(solution)/shard_map/back_transform/pallas_call | solution.py:448
  269.2 3.0 %copy.7 = f32[2048,256]{1,0:T(8,128)} copy(f32[2048,256]{1,0:T(8,128)} %get-tuple-element.6) | data formatting | bytes 4194304
